TPU v7x, 32 devices: a whole 2x2x4 slice. The times are simulated.
32 devices in a mesh: rep: 4 (over y, x), cp: 8 (over z, core).
Axes of the slice: x: 2, y: 2, z: 4, core: 2. Of those that a mesh axis runs over, the one named last changes fastest.
Arguments:
- tokens: bfloat16 [4, 2048, 768], P('rep', 'cp'), may hold values from -6 to 6
- query_weight: bfloat16 [768, 768], P('cp'), may hold values from -0.3125 to 0.3125
- query_bias: bfloat16 [768], P('cp'), may hold values from -3 to 3
- key_weight: bfloat16 [768, 768], P('cp'), may hold values from -0.3125 to 0.3125
- value_weight: bfloat16 [768, 768], P('cp'), may hold values from -0.21875 to 0.21875
- value_bias: bfloat16 [768], P('cp'), may hold values from -3 to 3
- output_weight: bfloat16 [768, 768], P('cp'), may hold values from -1.5 to 1.5
- output_bias: bfloat16 [768], P('cp'), may hold values from -1.796875 to 1.796875
- first_gain: bfloat16 [768], P('cp'), may hold values from 0.099609375 to 1.8984375
- first_shift: bfloat16 [768], P('cp'), may hold values from -1.796875 to 1.796875
- up_weight: bfloat16 [768, 3072], P('cp'), may hold values from -0.21875 to 0.21875
- up_bias: bfloat16 [3072], P('cp'), may hold values from -3 to 3
- down_weight: bfloat16 [3072, 768], P('cp'), may hold values from -0.109375 to 0.109375
- down_bias: bfloat16 [768], P('cp'), may hold values from -1.796875 to 1.796875
- second_gain: bfloat16 [768], P('cp'), may hold values from 0.099609375 to 1.8984375
- second_shift: bfloat16 [768], P('cp'), may hold values from -1.796875 to 1.796875
- cotangent: float32 [4, 2048, 768], P('rep', 'cp'), may hold values from -18 to 18
Outputs:
- layer_out: float32 [4, 2048, 768], P('rep', 'cp')
- grad_tokens: float32 [4, 2048, 768], P('rep', 'cp')
- grad_query_weight: float32 [768, 768], P('cp')
- grad_query_bias: float32 [768], P('cp')
- grad_key_weight: float32 [768, 768], P('cp')
- grad_value_weight: float32 [768, 768], P('cp')
- grad_value_bias: float32 [768], P('cp')
- grad_output_weight: float32 [768, 768], P('cp')
- grad_output_bias: float32 [768], P('cp')
- grad_first_gain: float32 [768], P('cp')
- grad_first_shift: float32 [768], P('cp')
- grad_up_weight: float32 [768, 3072], P('cp')
- grad_up_bias: float32 [3072], P('cp')
- grad_down_weight: float32 [3072, 768], P('cp')
- grad_down_bias: float32 [768], P('cp')
- grad_second_gain: float32 [768], P('cp')
- grad_second_shift: float32 [768], P('cp')
- rms_values: float32 [1], replicated
All inputs are finite; a program needn't handle non-finite values.
Results may differ from a plain program's by a relative error of at most 0.025.
Values may be sent and summed in bfloat16 or wider, within the bound.
A program may use at most 192 MiB of HBM per device.

v0:
```python
import math
import jax
import jax.numpy as jnp
from jax import lax
from jax.sharding import PartitionSpec as P

H = 12
HD = 64
KEYB = 512
EPSILON = 1e-12


def for_sending(x):
    return jax.tree.map(lambda a: a.astype(jnp.bfloat16) if a.dtype == jnp.float32 else a, x)


def normalize(values, norm_gain, norm_shift):
    center = values - jnp.mean(values, axis=-1, keepdims=True)
    spread = jnp.mean(center * center, axis=-1, keepdims=True)
    return center * lax.rsqrt(spread + EPSILON) * norm_gain + norm_shift


def gelu_exact(values):
    return 0.5 * values * (1.0 + lax.erf(values * (1.0 / math.sqrt(2.0))))


def matmul(left, right):
    return jnp.dot(left, right, preferred_element_type=jnp.float32)


def over_rows(left, right):
    return jnp.einsum("ta,tb->ab", left, right, preferred_element_type=jnp.float32)


def against(left, right):
    return jnp.einsum("ta,ba->tb", left, right, preferred_element_type=jnp.float32)


def column_sum(values):
    return jnp.sum(values.astype(jnp.float32), axis=0)


def head_scores(query_heads, key_heads):
    raw_scores = jnp.einsum(
        "qhd,khd->hqk", query_heads, key_heads, preferred_element_type=jnp.float32
    )
    return raw_scores * (1.0 / math.sqrt(HD))


def probabilities(scores, row_top, row_total):
    return jnp.exp(scores - row_top[:, :, None]) / row_total[:, :, None]


def score_grads(query_heads, grad_heads, key_heads, value_heads, row_top, row_total, row_delta):
    probs = probabilities(head_scores(query_heads, key_heads), row_top, row_total)
    grad_probs = jnp.einsum(
        "qhd,khd->hqk", grad_heads, value_heads, preferred_element_type=jnp.float32
    )
    grad_scores = (probs * (grad_probs - row_delta[:, :, None]) * (1.0 / math.sqrt(HD))).astype(
        jnp.bfloat16
    )
    return (probs.astype(jnp.bfloat16), grad_scores)


def on_device(
    tokens,
    query_weight,
    query_bias,
    key_weight,
    value_weight,
    value_bias,
    output_weight,
    output_bias,
    first_gain,
    first_shift,
    up_weight,
    up_bias,
    down_weight,
    down_bias,
    second_gain,
    second_shift,
    cotangent,
):
    shards = (
        query_weight,
        query_bias,
        key_weight,
        value_weight,
        value_bias,
        output_weight,
        output_bias,
        first_gain,
        first_shift,
        up_weight,
        up_bias,
        down_weight,
        down_bias,
        second_gain,
        second_shift,
    )
    gathered = (
        lax.all_gather(shards[0], "cp", axis=0, tiled=True),
        lax.all_gather(shards[1], "cp", axis=0, tiled=True),
        lax.all_gather(shards[2], "cp", axis=0, tiled=True),
        lax.all_gather(shards[3], "cp", axis=0, tiled=True),
        lax.all_gather(shards[4], "cp", axis=0, tiled=True),
        lax.all_gather(shards[5], "cp", axis=0, tiled=True),
        lax.all_gather(shards[6], "cp", axis=0, tiled=True),
        lax.all_gather(shards[7], "cp", axis=0, tiled=True),
        lax.all_gather(shards[8], "cp", axis=0, tiled=True),
        lax.all_gather(shards[9], "cp", axis=0, tiled=True),
        lax.all_gather(shards[10], "cp", axis=0, tiled=True),
        lax.all_gather(shards[11], "cp", axis=0, tiled=True),
        lax.all_gather(shards[12], "cp", axis=0, tiled=True),
        lax.all_gather(shards[13], "cp", axis=0, tiled=True),
        lax.all_gather(shards[14], "cp", axis=0, tiled=True),
    )
    (
        w_query,
        b_query,
        w_key,
        w_value,
        b_value,
        w_output,
        b_output,
        gain_first,
        shift_first,
        w_up,
        b_up,
        w_down,
        b_down,
        gain_second,
        shift_second,
    ) = gathered
    row_count = tokens.shape[1]
    model_width = tokens.shape[2]
    local_tokens = tokens[0]
    query_rows = (matmul(local_tokens, w_query) + b_query.astype(jnp.float32)).astype(jnp.bfloat16)
    key_rows = matmul(local_tokens, w_key).astype(jnp.bfloat16)
    value_rows = (matmul(local_tokens, w_value) + b_value.astype(jnp.float32)).astype(jnp.bfloat16)
    all_keys, all_values = (
        lax.all_gather(key_rows, "cp", axis=0, tiled=True),
        lax.all_gather(value_rows, "cp", axis=0, tiled=True),
    )
    seq_len = all_keys.shape[0]
    block_len = math.gcd(seq_len, KEYB)
    key_blocks = all_keys.reshape(seq_len // block_len, block_len, H, HD)
    value_blocks = all_values.reshape(seq_len // block_len, block_len, H, HD)
    query_heads = query_rows.reshape(row_count, H, HD)

    def stat_step(carry, key_block):
        old_top, old_total = carry
        scores = head_scores(query_heads, key_block)
        new_top = jnp.maximum(old_top, jnp.max(scores, axis=-1))
        new_total = old_total * jnp.exp(old_top - new_top) + jnp.sum(
            jnp.exp(scores - new_top[:, :, None]), axis=-1
        )
        return ((new_top, new_total), None)

    start_top = jnp.full((H, row_count), -jnp.inf, jnp.float32)
    start_total = jnp.zeros((H, row_count), jnp.float32)
    (row_top, row_total), _ = lax.scan(stat_step, (start_top, start_total), key_blocks)

    def value_step(carry, blocks):
        key_block, value_block = blocks
        probs = probabilities(head_scores(query_heads, key_block), row_top, row_total).astype(
            jnp.bfloat16
        )
        return (
            carry
            + jnp.einsum("hqk,khd->qhd", probs, value_block, preferred_element_type=jnp.float32),
            None,
        )

    head_zeros = jnp.zeros((row_count, H, HD), jnp.float32)
    context, _ = lax.scan(value_step, head_zeros, (key_blocks, value_blocks))
    context_low = context.reshape(row_count, model_width).astype(jnp.bfloat16)
    attn_out = matmul(context_low, w_output) + b_output.astype(jnp.float32)
    resid_first = local_tokens.astype(jnp.float32) + attn_out
    gain_one = gain_first.astype(jnp.float32)
    shift_one = shift_first.astype(jnp.float32)
    first_norm = normalize(resid_first, gain_one, shift_one)
    first_low = first_norm.astype(jnp.bfloat16)
    inner_act = matmul(first_low, w_up) + b_up.astype(jnp.float32)
    hidden_low = gelu_exact(inner_act).astype(jnp.bfloat16)
    resid_second = first_norm + (matmul(hidden_low, w_down) + b_down.astype(jnp.float32))
    gain_two = gain_second.astype(jnp.float32)
    shift_two = shift_second.astype(jnp.float32)
    layer_out = normalize(resid_second, gain_two, shift_two)
    backward_set = (
        lax.all_gather(shards[0], "cp", axis=0, tiled=True),
        lax.all_gather(shards[1], "cp", axis=0, tiled=True),
        lax.all_gather(shards[2], "cp", axis=0, tiled=True),
        lax.all_gather(shards[3], "cp", axis=0, tiled=True),
        lax.all_gather(shards[4], "cp", axis=0, tiled=True),
        lax.all_gather(shards[5], "cp", axis=0, tiled=True),
        lax.all_gather(shards[6], "cp", axis=0, tiled=True),
        lax.all_gather(shards[7], "cp", axis=0, tiled=True),
        lax.all_gather(shards[8], "cp", axis=0, tiled=True),
        lax.all_gather(shards[9], "cp", axis=0, tiled=True),
        lax.all_gather(shards[10], "cp", axis=0, tiled=True),
        lax.all_gather(shards[11], "cp", axis=0, tiled=True),
        lax.all_gather(shards[12], "cp", axis=0, tiled=True),
        lax.all_gather(shards[13], "cp", axis=0, tiled=True),
        lax.all_gather(shards[14], "cp", axis=0, tiled=True),
    )
    (
        back_query,
        back_qbias,
        back_key,
        back_value,
        back_vbias,
        back_output,
        back_obias,
        back_gain1,
        back_shift1,
        back_up,
        back_ubias,
        back_down,
        back_dbias,
        back_gain2,
        back_shift2,
    ) = backward_set
    _, pull_second = jax.vjp(
        normalize, resid_second, back_gain2.astype(jnp.float32), back_shift2.astype(jnp.float32)
    )
    grad_resid2, grad_gain2, grad_shift2 = pull_second(cotangent[0])
    grad_outer = grad_resid2.astype(jnp.bfloat16)
    grad_down_bias = column_sum(grad_outer)
    grad_down_weight = over_rows(hidden_low, grad_outer)
    grad_hidden = against(grad_outer, back_down)
    _, pull_gelu = jax.vjp(gelu_exact, inner_act)
    grad_inner = pull_gelu(grad_hidden)[0].astype(jnp.bfloat16)
    grad_up_bias = column_sum(grad_inner)
    grad_up_weight = over_rows(first_low, grad_inner)
    grad_first = grad_resid2 + against(grad_inner, back_up)
    _, pull_first = jax.vjp(
        normalize, resid_first, back_gain1.astype(jnp.float32), back_shift1.astype(jnp.float32)
    )
    grad_resid1, grad_gain1, grad_shift1 = pull_first(grad_first)
    grad_attn = grad_resid1.astype(jnp.bfloat16)
    grad_output_bias = column_sum(grad_attn)
    grad_output_weight = over_rows(context_low, grad_attn)
    grad_context = against(grad_attn, back_output).astype(jnp.bfloat16)
    grad_heads = grad_context.reshape(row_count, H, HD)
    row_delta = jnp.sum(grad_heads.astype(jnp.float32) * context, axis=-1).T

    def key_step(carry, blocks):
        key_block, value_block = blocks
        probs_low, grad_scores = score_grads(
            query_heads, grad_heads, key_block, value_block, row_top, row_total, row_delta
        )
        new_carry = carry + jnp.einsum(
            "hqk,khd->qhd", grad_scores, key_block, preferred_element_type=jnp.float32
        )
        key_part = jnp.einsum(
            "hqk,qhd->khd", grad_scores, query_heads, preferred_element_type=jnp.float32
        )
        value_part = jnp.einsum(
            "hqk,qhd->khd", probs_low, grad_heads, preferred_element_type=jnp.float32
        )
        joined = jnp.concatenate(
            [key_part.reshape(block_len, model_width), value_part.reshape(block_len, model_width)],
            axis=1,
        )
        return (new_carry, joined)

    grad_query_heads, key_terms = lax.scan(key_step, head_zeros, (key_blocks, value_blocks))
    key_pair = lax.psum_scatter(
        key_terms.reshape(seq_len, 2 * model_width).astype(jnp.bfloat16),
        "cp",
        scatter_dimension=0,
        tiled=True,
    ).astype(jnp.float32)
    grad_key_rows = key_pair[:, :model_width]
    grad_value_rows = key_pair[:, model_width:]
    grad_query_low = grad_query_heads.reshape(row_count, model_width).astype(jnp.bfloat16)
    grad_key_low = grad_key_rows.astype(jnp.bfloat16)
    grad_value_low = grad_value_rows.astype(jnp.bfloat16)
    grad_query_weight = over_rows(local_tokens, grad_query_low)
    grad_query_bias = column_sum(grad_query_low)
    grad_key_weight = over_rows(local_tokens, grad_key_low)
    grad_value_weight = over_rows(local_tokens, grad_value_low)
    grad_value_bias = column_sum(grad_value_low)
    grad_tokens = (
        grad_resid1
        + against(grad_query_low, back_query)
        + against(grad_key_low, back_key)
        + against(grad_value_low, back_value)
    )
    input_sq = jnp.sum(grad_tokens * grad_tokens)
    grads = (
        grad_query_weight,
        grad_query_bias,
        grad_key_weight,
        grad_value_weight,
        grad_value_bias,
        grad_output_weight,
        grad_output_bias,
        grad_gain1,
        grad_shift1,
        grad_up_weight,
        grad_up_bias,
        grad_down_weight,
        grad_down_bias,
        grad_gain2,
        grad_shift2,
    )
    summed = (
        lax.psum_scatter(
            grads[0].astype(jnp.bfloat16), "cp", scatter_dimension=0, tiled=True
        ).astype(jnp.float32),
        lax.psum_scatter(
            grads[1].astype(jnp.bfloat16), "cp", scatter_dimension=0, tiled=True
        ).astype(jnp.float32),
        lax.psum_scatter(
            grads[2].astype(jnp.bfloat16), "cp", scatter_dimension=0, tiled=True
        ).astype(jnp.float32),
        lax.psum_scatter(
            grads[3].astype(jnp.bfloat16), "cp", scatter_dimension=0, tiled=True
        ).astype(jnp.float32),
        lax.psum_scatter(
            grads[4].astype(jnp.bfloat16), "cp", scatter_dimension=0, tiled=True
        ).astype(jnp.float32),
        lax.psum_scatter(
            grads[5].astype(jnp.bfloat16), "cp", scatter_dimension=0, tiled=True
        ).astype(jnp.float32),
        lax.psum_scatter(
            grads[6].astype(jnp.bfloat16), "cp", scatter_dimension=0, tiled=True
        ).astype(jnp.float32),
        lax.psum_scatter(
            grads[7].astype(jnp.bfloat16), "cp", scatter_dimension=0, tiled=True
        ).astype(jnp.float32),
        lax.psum_scatter(
            grads[8].astype(jnp.bfloat16), "cp", scatter_dimension=0, tiled=True
        ).astype(jnp.float32),
        lax.psum_scatter(
            grads[9].astype(jnp.bfloat16), "cp", scatter_dimension=0, tiled=True
        ).astype(jnp.float32),
        lax.psum_scatter(
            grads[10].astype(jnp.bfloat16), "cp", scatter_dimension=0, tiled=True
        ).astype(jnp.float32),
        lax.psum_scatter(
            grads[11].astype(jnp.bfloat16), "cp", scatter_dimension=0, tiled=True
        ).astype(jnp.float32),
        lax.psum_scatter(
            grads[12].astype(jnp.bfloat16), "cp", scatter_dimension=0, tiled=True
        ).astype(jnp.float32),
        lax.psum_scatter(
            grads[13].astype(jnp.bfloat16), "cp", scatter_dimension=0, tiled=True
        ).astype(jnp.float32),
        lax.psum_scatter(
            grads[14].astype(jnp.bfloat16), "cp", scatter_dimension=0, tiled=True
        ).astype(jnp.float32),
    )
    carried = ()
    reduced = jax.tree.map(
        lambda part: part.astype(jnp.float32), lax.psum(for_sending(tuple(summed) + carried), "rep")
    )
    input_total = lax.psum(input_sq, ("rep", "cp"))
    count_entries = lax.axis_size("rep") * lax.axis_size("cp") * row_count * model_width
    rms_values = jnp.sqrt(jnp.stack([input_total / count_entries]))
    return (
        layer_out[None],
        grad_tokens[None],
        reduced[0],
        reduced[1],
        reduced[2],
        reduced[3],
        reduced[4],
        reduced[5],
        reduced[6],
        reduced[7],
        reduced[8],
        reduced[9],
        reduced[10],
        reduced[11],
        reduced[12],
        reduced[13],
        reduced[14],
        rms_values,
    )


def solution(mesh):
    in_specs = (
        P("rep", "cp", None),
        P("cp", None),
        P("cp"),
        P("cp", None),
        P("cp", None),
        P("cp"),
        P("cp", None),
        P("cp"),
        P("cp"),
        P("cp"),
        P("cp", None),
        P("cp"),
        P("cp", None),
        P("cp"),
        P("cp"),
        P("cp"),
        P("rep", "cp", None),
    )
    out_specs = (
        P("rep", "cp", None),
        P("rep", "cp", None),
        P("cp", None),
        P("cp"),
        P("cp", None),
        P("cp", None),
        P("cp"),
        P("cp", None),
        P("cp"),
        P("cp"),
        P("cp"),
        P("cp", None),
        P("cp"),
        P("cp", None),
        P("cp"),
        P("cp"),
        P("cp"),
        P(),
    )
    return jax.shard_map(
        on_device, mesh=mesh, in_specs=in_specs, out_specs=out_specs, check_vma=False
    )
```

profile of v0, /device:TPU:0, one launch (start us, length us, event | category | flops | bytes accessed | tf_op | source)
XLA Modules:
  0.0 778.3 jit_solution(13814633855772910897)
XLA Ops:
  17.3 30.8 %all-reduce.18 = (bf16[768]{0:T(1024)(128)(2,1)S(1)}, bf16[768]{0:T(1024)(128)(2,1)S(1)}, bf16[768]{0:T(1024)(128)(2,1)S(1)}, bf16[768]{0:T(1024)(128)(2,1)S(1)}...) all-reduce(bf16[768]{0:T(1024)(128)(2,1)S(1)} %dynamic-update-slice, ...), channel_id=1, replica_groups=mesh['rep'=4,'cp'=8] {'cp'}, use_global_device_ids=true, to_apply=%add.1 | all-reduce | flops 5376 | bytes 21504
  50.8 8.6 %all-gather.14.cloned.1.call-done = bf16[768,768]{1,0:T(8,128)(2,1)} async-done(((bf16[96,768]{1,0:T(8,128)(2,1)}), bf16[768,768]{1,0:T(8,128)(2,1)}) %all-gather.14.cloned.1.call-update) | async-done | bytes 1179664 | tf_op jit(solution)/shard_map/all_gather | solution.py:104
  67.2 12.8 %all-gather = bf16[8,1,384]{2,1,0:T(2,128)(2,1)S(1)} all-gather(bf16[1,1,384]{2,1,0:T(2,128)(2,1)S(1)} %reshape.166), channel_id=1, replica_groups=mesh['rep'=4,'cp'=8] {'cp'}, dimensions={0}, use_global_device_ids=true | all-gather | bytes 6912 | tf_op jit(solution)/shard_map/all_gather | solution.py:112
  85.5 38.1 %all-gather.12.cloned.1.call-done = bf16[2048,768]{1,0:T(8,128)(2,1)} async-done(((bf16[256,768]{1,0:T(8,128)(2,1)}), bf16[2048,768]{1,0:T(8,128)(2,1)}) %all-gather.12.cloned.1.call-update) | async-done | bytes 3145744 | tf_op jit(solution)/shard_map/all_gather | solution.py:143
  130.8 4.5 copy.64
  135.2 27.6 %all-gather.16.cloned.1.call-done = bf16[2048,768]{1,0:T(8,128)(2,1)} async-done(((bf16[256,768]{1,0:T(8,128)(2,1)}), bf16[2048,768]{1,0:T(8,128)(2,1)}) %all-gather.16.cloned.1.call-update) | async-done | bytes 3145744 | tf_op jit(solution)/shard_map/all_gather | solution.py:142
  172.7 13.2 %while.37 = (s32[]{:T(128)}, f32[12,256]{1,0:T(8,128)S(1)}, f32[12,256]{1,0:T(8,128)}, bf16[4,512,12,64]{1,3,2,0:T(8,128)(2,1)S(1)}, bf16[256,12,64]{0,2,1:T(8,128)(2,1)S(1)}, /*index=5*/s32[]{:T(128)}, s32[]{:T(128)}) while((s32[]{:T(128)}, f32[12,256]{1,0:T(8,128)S(1)}, f32[12,256]{1,0:T(8,128)}, ...), condition=%wide.region_3.4_spmd.clone, body=%wide.region_0.3_spmd.clone.sunk | while | flops 209206272 | bytes 13922404 | solution.py:162
  185.9 16.7 %while.38 = (s32[]{:T(128)}, f32[256,12,64]{0,2,1:T(8,128)}, bf16[4,512,12,64]{1,3,2,0:T(8,128)(2,1)}, bf16[4,512,12,64]{1,3,2,0:T(8,128)(2,1)S(1)}, bf16[256,12...) while((s32[]{:T(128)}, f32[256,12,64]{0,2,1:T(8,128)}, ...), condition=%wide.region_5.6_spmd.clone, body=%wide.region_4.5_spmd.clone.sunk | while | flops 409337856 | bytes 3573358 | solution.py:176
  211.0 27.6 %all-gather.22.cloned.1.call-done = bf16[768,3072]{1,0:T(8,128)(2,1)} async-done(((bf16[96,3072]{1,0:T(8,128)(2,1)}), bf16[768,3072]{1,0:T(8,128)(2,1)}) %all-gather.22.cloned.1.call-update) | async-done | bytes 4718608 | tf_op jit(solution)/shard_map/all_gather | solution.py:111
  238.6 6.6 multiply_convert_fusion.1
  245.1 45.1 %all-gather.24.cloned.1.call-done = bf16[3072,768]{1,0:T(8,128)(2,1)} async-done(((bf16[384,768]{1,0:T(8,128)(2,1)}), bf16[3072,768]{1,0:T(8,128)(2,1)}) %all-gather.24.cloned.1.call-update) | async-done | bytes 4718608 | tf_op jit(solution)/shard_map/all_gather | solution.py:113
  290.2 4.7 fusion.64
  309.3 46.7 %while.39 = (s32[]{:T(128)}, f32[256,12,64]{0,2,1:T(8,128)S(1)}, bf16[4,512,1536]{2,1,0:T(8,128)(2,1)}, bf16[4,512,12,64]{1,3,2,0:T(8,128)(2,1)}, bf16[256,12,64...) while((s32[]{:T(128)}, f32[256,12,64]{0,2,1:T(8,128)S(1)}, ...), condition=%wide.region_16.17_spmd.clone, body=%wide.region_15.16_spmd.clone.sunk | while | flops 1022754816 | bytes 54309124 | solution.py:268
  359.1 65.7 %reduce-scatter.14.cloned.1.call-done = bf16[256,1536]{1,0:T(8,128)(2,1)} async-done(((bf16[2048,1536]{1,0:T(8,128)(2,1)}), bf16[256,1536]{1,0:T(8,128)(2,1)}) %reduce-scatter.14.cloned.1.call-update) | async-done | bytes 786448 | tf_op jit(solution)/shard_map/reduce_scatter | solution.py:269
  431.9 4.9 convolution_convert_fusion.1
  441.9 16.9 %reduce-scatter.22.cloned.1.call-done = bf16[96,768]{1,0:T(8,128)(2,1)} async-done(((bf16[768,768]{1,0:T(8,128)(2,1)}), bf16[96,768]{1,0:T(8,128)(2,1)}) %reduce-scatter.22.cloned.1.call-update) | async-done | bytes 147472
  460.6 31.8 %reduce-scatter.26.cloned.1.call-done = bf16[96,768]{1,0:T(8,128)(2,1)} async-done(((bf16[768,768]{1,0:T(8,128)(2,1)}), bf16[96,768]{1,0:T(8,128)(2,1)}) %reduce-scatter.26.cloned.1.call-update) | async-done | bytes 147472
  494.1 32.0 %reduce-scatter.24.cloned.1.call-done = bf16[96,768]{1,0:T(8,128)(2,1)} async-done(((bf16[768,768]{1,0:T(8,128)(2,1)}), bf16[96,768]{1,0:T(8,128)(2,1)}) %reduce-scatter.24.cloned.1.call-update) | async-done | bytes 147472
  527.8 31.8 %reduce-scatter.16.cloned.1.call-done = bf16[96,768]{1,0:T(8,128)(2,1)} async-done(((bf16[768,768]{1,0:T(8,128)(2,1)}), bf16[96,768]{1,0:T(8,128)(2,1)}) %reduce-scatter.16.cloned.1.call-update) | async-done | bytes 147472 | tf_op jit(solution)/shard_map/reduce_scatter | solution.py:325
  559.6 55.3 %reduce-scatter.18.cloned.1.call-done = bf16[96,3072]{1,0:T(8,128)(2,1)} async-done(((bf16[768,3072]{1,0:T(8,128)(2,1)}), bf16[96,3072]{1,0:T(8,128)(2,1)}) %reduce-scatter.18.cloned.1.call-update) | async-done | bytes 589840 | tf_op jit(solution)/shard_map/reduce_scatter | solution.py:337
  614.9 55.5 %reduce-scatter.20.cloned.1.call-done = bf16[384,768]{1,0:T(8,128)(2,1)} async-done(((bf16[3072,768]{1,0:T(8,128)(2,1)}), bf16[384,768]{1,0:T(8,128)(2,1)}) %reduce-scatter.20.cloned.1.call-update) | async-done | bytes 589840 | tf_op jit(solution)/shard_map/reduce_scatter | solution.py:343
  677.9 38.4 %psum.127 = f32[]{:T(128)} all-reduce(f32[]{:T(128)} %get-tuple-element.440), channel_id=1, replica_groups=mesh['rep'=4,'cp'=8] {'rep','cp'}, use_global_device_ids=true, to_apply=%region_58.59 | all-reduce | flops 1 | bytes 8 | tf_op jit(solution)/shard_map/psum | solution.py:360
  717.2 26.8 %all-reduce.17 = (bf16[768]{0:T(1024)(128)(2,1)S(1)}, bf16[768]{0:T(1024)(128)(2,1)S(1)}, bf16[768]{0:T(1024)(128)(2,1)S(1)}, bf16[768]{0:T(1024)(128)(2,1)S(1)}...) all-reduce(bf16[768]{0:T(1024)(128)(2,1)S(1)} %copy-done.53, ...), channel_id=1, replica_groups=mesh['rep'=4,'cp'=8] {'cp'}, use_global_device_ids=true, to_apply=%add.7 | all-reduce | flops 9984 | bytes 39936
  744.7 9.9 %all-reduce.19 = (bf16[96]{0:T(256)(128)(2,1)S(1)}, bf16[96]{0:T(256)(128)(2,1)S(1)}, bf16[96]{0:T(256)(128)(2,1)S(1)}, bf16[96]{0:T(256)(128)(2,1)S(1)}, bf16[9...) all-reduce(bf16[96]{0:T(256)(128)(2,1)S(1)} %dynamic-slice.9, ...), channel_id=1, replica_groups=mesh['rep'=4,'cp'=8] {'rep'}, use_global_device_ids=true, to_apply=%region_22.23 | all-reduce | flops 1152 | bytes 4608 | tf_op jit(solution)/shard_map/psum | solution.py:358
  (352 shorter events, 184.3 us)
Async XLA Ops:
  7.2 40.9 %all-gather.10.cloned.1.call-start = ((), (), s32[]{:S(2)}) async-start(), calls=%async_computation.7 | async-start | bytes 1327104 | tf_op jit(solution)/shard_map/all_gather | solution.py:105
  7.9 51.5 %all-gather.14.cloned.1.call-start = ((), (), s32[]{:S(2)}) async-start(), calls=%async_computation.9 | async-start | bytes 1327104 | tf_op jit(solution)/shard_map/all_gather | solution.py:104
  8.7 74.9 %all-gather.18.cloned.1.call-start = ((), (), s32[]{:S(2)}) async-start(), calls=%async_computation.11 | async-start | bytes 1327104 | tf_op jit(solution)/shard_map/all_gather | solution.py:102
  9.4 114.2 %all-gather.12.cloned.1.call-start = ((), (), s32[]{:S(2)}) async-start(), calls=%async_computation.8 | async-start | bytes 3538944 | tf_op jit(solution)/shard_map/all_gather | solution.py:143
  50.8 112.0 %all-gather.16.cloned.1.call-start = ((), (), s32[]{:S(2)}) async-start(), calls=%async_computation.10 | async-start | bytes 3538944 | tf_op jit(solution)/shard_map/all_gather | solution.py:142
  62.0 143.1 %all-gather.20.cloned.1.call-start = ((), (), s32[]{:S(2)}) async-start(), calls=%async_computation.12 | async-start | bytes 1327104 | tf_op jit(solution)/shard_map/all_gather | solution.py:107
  62.6 176.0 %all-gather.22.cloned.1.call-start = ((), (), s32[]{:S(2)}) async-start(), calls=%async_computation.13 | async-start | bytes 5308416 | tf_op jit(solution)/shard_map/all_gather | solution.py:111
  63.3 226.9 %all-gather.24.cloned.1.call-start = ((), (), s32[]{:S(2)}) async-start(), calls=%async_computation.14 | async-start | bytes 5308416 | tf_op jit(solution)/shard_map/all_gather | solution.py:113
  64.1 360.7 %reduce-scatter.14.cloned.1.call-start = ((), (), s32[]{:S(2)}) async-start(), calls=%async_computation.15 | async-start | bytes 7077888 | tf_op jit(solution)/shard_map/reduce_scatter | solution.py:269
  202.6 92.3 %copy-start.2 = (bf16[4,512,12,64]{1,3,2,0:T(8,128)(2,1)}, bf16[4,512,12,64]{1,3,2,0:T(8,128)(2,1)S(1)}, u32[]{:S(2)}) copy-start(bf16[4,512,12,64]{1,3,2,0:T(8,128)(2,1)S(1)} %get-tuple-element.695) | copy-start | bytes 9437188
  356.1 102.8 %reduce-scatter.22.cloned.1.call-start = ((), (), s32[]{:S(2)}) async-start(), calls=%async_computation.19 | async-start | bytes 1327104
  359.0 133.4 %reduce-scatter.26.cloned.1.call-start = ((), (), s32[]{:S(2)}) async-start(), calls=%async_computation.21 | async-start | bytes 1327104
  427.9 98.3 %reduce-scatter.24.cloned.1.call-start = ((), (), s32[]{:S(2)}) async-start(), calls=%async_computation.20 | async-start | bytes 1327104
  430.0 129.7 %reduce-scatter.16.cloned.1.call-start = ((), (), s32[]{:S(2)}) async-start(), calls=%async_computation.16 | async-start | bytes 1327104 | tf_op jit(solution)/shard_map/reduce_scatter | solution.py:325
  431.5 183.4 %reduce-scatter.18.cloned.1.call-start = ((), (), s32[]{:S(2)}) async-start(), calls=%async_computation.17 | async-start | bytes 5308416 | tf_op jit(solution)/shard_map/reduce_scatter | solution.py:337
  436.8 233.7 %reduce-scatter.20.cloned.1.call-start = ((), (), s32[]{:S(2)}) async-start(), calls=%async_computation.18 | async-start | bytes 5308416 | tf_op jit(solution)/shard_map/reduce_scatter | solution.py:343
  441.9 229.9 %copy-start.11 = (f32[1,256,768]{2,1,0:T(8,128)S(1)}, f32[1,256,768]{2,1,0:T(8,128)}, u32[]{:S(2)}) copy-start(f32[1,256,768]{2,1,0:T(8,128)} %param.39) | copy-start | bytes 2359300
  441.9 230.6 %copy-start.58 = (bf16[96]{0:T(256)(128)(2,1)S(1)}, bf16[96]{0:T(256)(128)(2,1)}, u32[]{:S(2)}) copy-start(bf16[96]{0:T(256)(128)(2,1)} %param.38) | copy-start | bytes 580
  441.9 231.4 %copy-start.13 = (f32[256,768]{1,0:T(8,128)S(1)}, f32[256,768]{1,0:T(8,128)}, u32[]{:S(2)}) copy-start(f32[256,768]{1,0:T(8,128)} %copy-done.12) | copy-start | bytes 2359300
  441.9 231.4 %copy-start.46 = (f32[256]{0:T(256)S(1)}, f32[256]{0:T(256)}, u32[]{:S(2)}) copy-start(f32[256]{0:T(256)} %copy-done.45) | copy-start | bytes 3076
  441.9 318.4 %all-reduce.23.cloned.1.call-start = ((), (), s32[]{:S(2)}) async-start(), calls=%async_computation.22 | async-start | bytes 3833856 | tf_op jit(solution)/shard_map/psum | solution.py:358
  494.1 181.2 %copy-start.15 = (bf16[768,768]{1,0:T(8,128)(2,1)S(1)}, bf16[768,768]{1,0:T(8,128)(2,1)}, u32[]{:S(2)}) copy-start(bf16[768,768]{1,0:T(8,128)(2,1)} %all-gather.14.cloned.1.call-done) | copy-start | bytes 3538948
  675.3 83.9 %copy-start.7 = (f32[256,768]{1,0:T(8,128)S(1)}, f32[256,768]{1,0:T(8,128)}, u32[]{:S(2)}) copy-start(f32[256,768]{1,0:T(8,128)} %copy-done.6) | copy-start | bytes 2359300
  675.3 83.9 %copy-start.33 = (f32[768]{0:T(1024)S(1)}, f32[768]{0:T(1024)}, u32[]{:S(2)}) copy-start(f32[768]{0:T(1024)} %convert_element_type.231) | copy-start | bytes 9220
  (68 other events, 770.7 us)
Sparse Core Ops, SparseCore 0:
  9.6 25.6 all-gather.9
  36.9 22.4 all-gather.13
  61.1 22.4 all-gather.17
  85.7 37.8 all-gather.11
  125.7 37.1 all-gather.15
  164.3 21.6 all-gather.19
  187.7 50.8 all-gather.21
  240.2 49.9 all-gather.23
  356.2 68.4 reduce-scatter.13
  427.4 31.3 reduce-scatter.21
  461.2 31.1 reduce-scatter.25
  495.1 30.9 reduce-scatter.23
  528.4 31.1 reduce-scatter.15
  561.8 53.0 reduce-scatter.17
  617.1 53.3 reduce-scatter.19
  674.7 66.5 all-reduce.22
where the time goes:
time: 780 us; the launch traced here: 778 us
  waiting for transfers between devices  443 us (57%)
  blocking collectives  119 us (15%)
  matrix products  103 us (13%)
  local copies, waits for them, and re-layouts  59.7 us (8%)
  other arithmetic  34 us (4%)
  between operations  18.6 us (2%)
    unnamed x19, waiting for transfers between devices  84.9 us
    reduce_scatter x1, waiting for transfers between devices, on_device(): lax.psum_scatter(key_terms.reshape(seq_len, 2 * model_width).astype(jnp.b...  65.7 us
    unnamed x2, blocking collectives  57.6 us
    reduce_scatter x1, waiting for transfers between devices, on_device(): lax.psum_scatter(grads[11].astype(jnp.bfloat16), 'cp', scatter_dimension=...  55.5 us
    reduce_scatter x1, waiting for transfers between devices, on_device(): lax.psum_scatter(grads[9].astype(jnp.bfloat16), 'cp', scatter_dimension=0...  55.3 us
    all_gather x1, waiting for transfers between devices, on_device(): lax.all_gather(shards[11], 'cp', axis=0, tiled=True)  45.1 us
    psum x1, blocking collectives, on_device(): input_total = lax.psum(input_sq, ('rep', 'cp'))  38.4 us
    all_gather x1, waiting for transfers between devices, on_device(): lax.all_gather(value_rows, 'cp', axis=0, tiled=True)  38.1 us
  transfers between devices with their start and end apart: 16, of which 13 were waited for; matrix products, arithmetic and copies ran while one was open for 15% of the time, Pallas kernels for 0%

commit v1 on v0

--- a/solution.py
+++ b/solution.py
@@ -8,6 +8,17 @@
 HD = 64
 KEYB = 512
 EPSILON = 1e-12
+
+
+def gather_around(value, axis, dim):
+    ways = lax.axis_size(axis)
+    pieces = [value]
+    for far in range(1, ways):
+        pieces.append(
+            lax.ppermute(pieces[far - 1], axis, [(d, (d - 1) % ways) for d in range(ways)])
+        )
+    line = jnp.concatenate(pieces, axis=dim)
+    return jnp.roll(line, lax.axis_index(axis) * value.shape[dim], axis=dim)
 
 
 def for_sending(x):
@@ -139,7 +150,7 @@
     key_rows = matmul(local_tokens, w_key).astype(jnp.bfloat16)
     value_rows = (matmul(local_tokens, w_value) + b_value.astype(jnp.float32)).astype(jnp.bfloat16)
     all_keys, all_values = (
-        lax.all_gather(key_rows, "cp", axis=0, tiled=True),
+        gather_around(key_rows, "cp", 0),
         lax.all_gather(value_rows, "cp", axis=0, tiled=True),
     )
     seq_len = all_keys.shape[0]

time: 780 us -> 776 us (level)
  waiting for transfers between devices: 443 us -> 350 us
  starting transfers between devices: 0.9 us -> 24.9 us
  matrix products: 103 us -> 126 us
  local copies, waits for them, and re-layouts: 59.7 us -> 81.8 us
  other arithmetic: 34 us -> 48 us
    ppermute x0 -> x7, waiting for transfers between devices: none -> 42.6 us  [gather_around(): lax.ppermute(pieces[far - 1], axis, [(d, (d - 1) % ways) for d in range(w...]
    all_gather x1, waiting for transfers between devices: 38.1 us -> 0.01 us  [on_device(): lax.all_gather(value_rows, 'cp', axis=0, tiled=True)]
    all_gather x1, waiting for transfers between devices: 45.1 us -> 9.69 us  [on_device(): lax.all_gather(shards[11], 'cp', axis=0, tiled=True)]
    all_gather x1 -> x0, waiting for transfers between devices: 27.6 us -> none  [on_device(): lax.all_gather(key_rows, 'cp', axis=0, tiled=True)]
    all_gather x1, waiting for transfers between devices: 27.6 us -> 0.02 us  [on_device(): lax.all_gather(shards[9], 'cp', axis=0, tiled=True)]
    ppermute x0 -> x7, starting transfers between devices: none -> 24 us  [gather_around(): lax.ppermute(pieces[far - 1], axis, [(d, (d - 1) % ways) for d in range(w...]
    dot_general x8, matrix products: 15.1 us -> 30.4 us  [head_scores(): jnp.einsum('qhd,khd->hqk', query_heads, key_heads, preferred_element_type...]
    dynamic_update_slice x8, local copies, waits for them, and re-layouts: 7.96 us -> 21.1 us  [on_device(): lax.scan(key_step, head_zeros, (key_blocks, value_blocks))]
  transfers between devices with their start and end apart: 16 -> 22, of which waited for: 13 -> 15; matrix products, arithmetic and copies ran while one was open for 15% -> 20% of each run, Pallas kernels for 0% -> 0%
where the time goes in v1:
time: 776 us; the launch traced here: 773 us
  waiting for transfers between devices  350 us (45%)
  matrix products  126 us (16%)
  blocking collectives  124 us (16%)
  local copies, waits for them, and re-layouts  81.8 us (11%)
  other arithmetic  48 us (6%)
  starting transfers between devices  24.9 us (3%)
  between operations  18.6 us (2%)
    unnamed x18, waiting for transfers between devices  83 us
    reduce_scatter x1, waiting for transfers between devices, on_device(): lax.psum_scatter(key_terms.reshape(seq_len, 2 * model_width).astype(jnp.b...  64.6 us
    unnamed x2, blocking collectives  57.6 us
    reduce_scatter x1, waiting for transfers between devices, on_device(): lax.psum_scatter(grads[9].astype(jnp.bfloat16), 'cp', scatter_dimension=0...  55.5 us
    reduce_scatter x1, waiting for transfers between devices, on_device(): lax.psum_scatter(grads[11].astype(jnp.bfloat16), 'cp', scatter_dimension=...  55.4 us
    ppermute x7, waiting for transfers between devices, gather_around(): lax.ppermute(pieces[far - 1], axis, [(d, (d - 1) % ways) for d in range(w...  42.6 us
    unnamed x178, local copies, waits for them, and re-layouts  41 us
    psum x1, blocking collectives, on_device(): input_total = lax.psum(input_sq, ('rep', 'cp'))  38.4 us
  transfers between devices with their start and end apart: 22, of which 15 were waited for; matrix products, arithmetic and copies ran while one was open for 20% of the time, Pallas kernels for 0%

profile of v1, /device:TPU:0, one launch (start us, length us, event | category | flops | bytes accessed | tf_op | source)
XLA Modules:
  0.0 773.3 jit_solution(4608198820472222871)
XLA Ops:
  17.3 30.8 %all-reduce.18 = (bf16[768]{0:T(1024)(128)(2,1)S(1)}, bf16[768]{0:T(1024)(128)(2,1)S(1)}, bf16[768]{0:T(1024)(128)(2,1)S(1)}, bf16[768]{0:T(1024)(128)(2,1)S(1)}...) all-reduce(bf16[768]{0:T(1024)(128)(2,1)S(1)} %dynamic-update-slice, ...), channel_id=1, replica_groups=mesh['rep'=4,'cp'=8] {'cp'}, use_global_device_ids=true, to_apply=%add.1 | all-reduce | flops 5376 | bytes 21504
  52.0 7.4 all-gather.13.cloned.1.call-done
  64.0 6.4 collective-permute-done
  74.2 9.2 %collective-permute-done.1 = bf16[256,768]{1,0:T(8,128)(2,1)S(1)} collective-permute-done((bf16[256,768]{1,0:T(8,128)(2,1)S(1)}, bf16[256,768]{1,0:T(8,128)(2,1)S(1)}, u32[]{:S(2)}, u32[]{:S(2)}) %collective-permute-start.1) | collective-permute-done | bytes 393248 | tf_op jit(solution)/shard_map/ppermute | solution.py:18
  87.1 5.3 collective-permute-done.2
  96.1 13.6 %collective-permute-done.3 = bf16[256,768]{1,0:T(8,128)(2,1)S(1)} collective-permute-done((bf16[256,768]{1,0:T(8,128)(2,1)S(1)}, bf16[256,768]{1,0:T(8,128)(2,1)S(1)}, u32[]{:S(2)}, u32[]{:S(2)}) %collective-permute-start.3) | collective-permute-done | bytes 393248 | tf_op jit(solution)/shard_map/ppermute | solution.py:18
  115.9 18.0 %all-gather = bf16[8,1,384]{2,1,0:T(2,128)(2,1)S(1)} all-gather(bf16[1,1,384]{2,1,0:T(2,128)(2,1)S(1)} %reshape.166), channel_id=1, replica_groups=mesh['rep'=4,'cp'=8] {'cp'}, dimensions={0}, use_global_device_ids=true | all-gather | bytes 6912 | tf_op jit(solution)/shard_map/all_gather | solution.py:123
  152.8 5.5 collective-permute-done.6
  177.8 39.8 %while.37 = (s32[]{:T(128)}, f32[12,256]{1,0:T(8,128)S(1)}, f32[12,256]{1,0:T(8,128)}, bf16[4,512,12,64]{1,3,2,0:T(8,128)(2,1)}, bf16[256,12,64]{0,2,1:T(8,128)(2,1)}, /*index=5*/s32[]{:T(128)}, s32[]{:T(128)}) while((s32[]{:T(128)}, f32[12,256]{1,0:T(8,128)S(1)}, f32[12,256]{1,0:T(8,128)}, bf16[4,512,12,64]{1,3,2,0:T(8,128)(2,1)}, ...), condition=%wide.region_3.4_spmd.clone, body=%wide.region_0.3_spmd.clone.sunk | while | flops 209206272 | bytes 13922904 | solution.py:173
  227.4 17.1 %while.38 = (s32[]{:T(128)}, f32[256,12,64]{0,2,1:T(8,128)}, bf16[4,512,12,64]{1,3,2,0:T(8,128)(2,1)S(1)}, bf16[4,512,12,64]{1,3,2,0:T(8,128)(2,1)}, bf16[256,12...) while((s32[]{:T(128)}, f32[256,12,64]{0,2,1:T(8,128)}, ...), condition=%wide.region_5.6_spmd.clone, body=%wide.region_4.5_spmd.clone.sunk | while | flops 409337856 | bytes 3572839 | solution.py:187
  250.2 6.6 multiply_convert_fusion.1
  256.8 9.7 %all-gather.21.cloned.1.call-done = bf16[3072,768]{1,0:T(8,128)(2,1)} async-done(((bf16[384,768]{1,0:T(8,128)(2,1)}), bf16[3072,768]{1,0:T(8,128)(2,1)}) %all-gather.21.cloned.1.call-update) | async-done | bytes 4718608 | tf_op jit(solution)/shard_map/all_gather | solution.py:124
  282.8 70.2 %while.39 = (s32[]{:T(128)}, f32[256,12,64]{0,2,1:T(8,128)}, bf16[4,512,1536]{2,1,0:T(8,128)(2,1)}, bf16[4,512,12,64]{1,3,2,0:T(8,128)(2,1)}, bf16[256,12,64]{0,...) while((s32[]{:T(128)}, f32[256,12,64]{0,2,1:T(8,128)}, ...), condition=%wide.region_16.17_spmd.clone, body=%wide.region_15.16_spmd.clone.sunk | while | flops 1022754816 | bytes 44918936 | solution.py:279
  357.0 64.6 %reduce-scatter.14.cloned.1.call-done = bf16[256,1536]{1,0:T(8,128)(2,1)} async-done(((bf16[2048,1536]{1,0:T(8,128)(2,1)}), bf16[256,1536]{1,0:T(8,128)(2,1)}) %reduce-scatter.14.cloned.1.call-update) | async-done | bytes 786448 | tf_op jit(solution)/shard_map/reduce_scatter | solution.py:280
  434.9 5.2 convolution_convert_fusion.1
  440.2 15.8 %reduce-scatter.22.cloned.1.call-done = bf16[96,768]{1,0:T(8,128)(2,1)} async-done(((bf16[768,768]{1,0:T(8,128)(2,1)}), bf16[96,768]{1,0:T(8,128)(2,1)}) %reduce-scatter.22.cloned.1.call-update) | async-done | bytes 147472
  457.7 32.1 %reduce-scatter.24.cloned.1.call-done = bf16[96,768]{1,0:T(8,128)(2,1)} async-done(((bf16[768,768]{1,0:T(8,128)(2,1)}), bf16[96,768]{1,0:T(8,128)(2,1)}) %reduce-scatter.24.cloned.1.call-update) | async-done | bytes 147472
  491.5 31.9 %reduce-scatter.26.cloned.1.call-done = bf16[96,768]{1,0:T(8,128)(2,1)} async-done(((bf16[768,768]{1,0:T(8,128)(2,1)}), bf16[96,768]{1,0:T(8,128)(2,1)}) %reduce-scatter.26.cloned.1.call-update) | async-done | bytes 147472
  525.1 31.8 %reduce-scatter.16.cloned.1.call-done = bf16[96,768]{1,0:T(8,128)(2,1)} async-done(((bf16[768,768]{1,0:T(8,128)(2,1)}), bf16[96,768]{1,0:T(8,128)(2,1)}) %reduce-scatter.16.cloned.1.call-update) | async-done | bytes 147472 | tf_op jit(solution)/shard_map/reduce_scatter | solution.py:336
  556.9 55.4 %reduce-scatter.20.cloned.1.call-done = bf16[384,768]{1,0:T(8,128)(2,1)} async-done(((bf16[3072,768]{1,0:T(8,128)(2,1)}), bf16[384,768]{1,0:T(8,128)(2,1)}) %reduce-scatter.20.cloned.1.call-update) | async-done | bytes 589840 | tf_op jit(solution)/shard_map/reduce_scatter | solution.py:354
  612.3 55.5 %reduce-scatter.18.cloned.1.call-done = bf16[96,3072]{1,0:T(8,128)(2,1)} async-done(((bf16[768,3072]{1,0:T(8,128)(2,1)}), bf16[96,3072]{1,0:T(8,128)(2,1)}) %reduce-scatter.18.cloned.1.call-update) | async-done | bytes 589840 | tf_op jit(solution)/shard_map/reduce_scatter | solution.py:348
  675.4 38.4 %psum.127 = f32[]{:T(128)} all-reduce(f32[]{:T(128)} %get-tuple-element.442), channel_id=1, replica_groups=mesh['rep'=4,'cp'=8] {'rep','cp'}, use_global_device_ids=true, to_apply=%region_58.59 | all-reduce | flops 1 | bytes 8 | tf_op jit(solution)/shard_map/psum | solution.py:371
  713.9 26.8 %all-reduce.17 = (bf16[768]{0:T(1024)(128)(2,1)S(1)}, bf16[768]{0:T(1024)(128)(2,1)S(1)}, bf16[768]{0:T(1024)(128)(2,1)S(1)}, bf16[768]{0:T(1024)(128)(2,1)S(1)}...) all-reduce(bf16[768]{0:T(1024)(128)(2,1)S(1)} %copy-done.52, ...), channel_id=1, replica_groups=mesh['rep'=4,'cp'=8] {'cp'}, use_global_device_ids=true, to_apply=%add.7 | all-reduce | flops 9984 | bytes 39936
  741.4 10.0 %all-reduce.19 = (bf16[96]{0:T(256)(128)(2,1)S(1)}, bf16[96]{0:T(256)(128)(2,1)S(1)}, bf16[96]{0:T(256)(128)(2,1)S(1)}, bf16[96]{0:T(256)(128)(2,1)S(1)}, bf16[9...) all-reduce(bf16[96]{0:T(256)(128)(2,1)S(1)} %dynamic-slice.9, ...), channel_id=1, replica_groups=mesh['rep'=4,'cp'=8] {'rep'}, use_global_device_ids=true, to_apply=%region_22.23 | all-reduce | flops 1152 | bytes 4608 | tf_op jit(solution)/shard_map/psum | solution.py:369
  (361 shorter events, 274.6 us)
Async XLA Ops:
  7.2 41.0 %all-gather.9.cloned.1.call-start = ((), (), s32[]{:S(2)}) async-start(), calls=%async_computation.7 | async-start | bytes 1327104 | tf_op jit(solution)/shard_map/all_gather | solution.py:116
  7.9 51.5 %all-gather.13.cloned.1.call-start = ((), (), s32[]{:S(2)}) async-start(), calls=%async_computation.9 | async-start | bytes 1327104 | tf_op jit(solution)/shard_map/all_gather | solution.py:115
  8.7 130.4 %all-gather.15.cloned.1.call-start = ((), (), s32[]{:S(2)}) async-start(), calls=%async_computation.10 | async-start | bytes 1327104 | tf_op jit(solution)/shard_map/all_gather | solution.py:113
  9.4 208.2 %all-gather.11.cloned.1.call-start = ((), (), s32[]{:S(2)}) async-start(), calls=%async_computation.8 | async-start | bytes 3538944 | tf_op jit(solution)/shard_map/all_gather | solution.py:154
  50.8 196.3 %all-gather.17.cloned.1.call-start = ((), (), s32[]{:S(2)}) async-start(), calls=%async_computation.11 | async-start | bytes 1327104 | tf_op jit(solution)/shard_map/all_gather | solution.py:118
  51.4 198.8 %all-gather.19.cloned.1.call-start = ((), (), s32[]{:S(2)}) async-start(), calls=%async_computation.12 | async-start | bytes 5308416 | tf_op jit(solution)/shard_map/all_gather | solution.py:122
  52.0 214.5 %all-gather.21.cloned.1.call-start = ((), (), s32[]{:S(2)}) async-start(), calls=%async_computation.13 | async-start | bytes 5308416 | tf_op jit(solution)/shard_map/all_gather | solution.py:124
  62.0 8.4 %collective-permute-start = (bf16[256,768]{1,0:T(8,128)(2,1)S(1)}, bf16[256,768]{1,0:T(8,128)(2,1)S(1)}, u32[]{:S(2)}, u32[]{:S(2)}) collective-permute-start(bf16[256,768]{1,0:T(8,128)(2,1)S(1)} %get-tuple-element.434), channel_id=1, source_target_pairs={{0,7},{1,0},{2,1},{3,2},{4,3},{5,4},{6,5},{7,6},{8,15},{9,8},{10,9... | collective-permute-start | bytes 1179656 | tf_op jit(solution)/shard_map/ppermute | solution.py:18
  70.4 12.9 %collective-permute-start.1 = (bf16[256,768]{1,0:T(8,128)(2,1)S(1)}, bf16[256,768]{1,0:T(8,128)(2,1)S(1)}, u32[]{:S(2)}, u32[]{:S(2)}) collective-permute-start(bf16[256,768]{1,0:T(8,128)(2,1)S(1)} %collective-permute-done), channel_id=1, source_target_pairs={{0,7},{1,0},{2,1},{3,2},{4,3},{5,4},{6,5},{7,6},{8,15},{9,8},{10,9... | collective-permute-start | bytes 1179656 | tf_op jit(solution)/shard_map/ppermute | solution.py:18
  83.4 9.0 %collective-permute-start.2 = (bf16[256,768]{1,0:T(8,128)(2,1)S(1)}, bf16[256,768]{1,0:T(8,128)(2,1)S(1)}, u32[]{:S(2)}, u32[]{:S(2)}) collective-permute-start(bf16[256,768]{1,0:T(8,128)(2,1)S(1)} %collective-permute-done.1), channel_id=1, source_target_pairs={{0,7},{1,0},{2,1},{3,2},{4,3},{5,4},{6,5},{7,6},{8,15},{9,8},{10,9... | collective-permute-start | bytes 1179656 | tf_op jit(solution)/shard_map/ppermute | solution.py:18
  92.4 17.3 %collective-permute-start.3 = (bf16[256,768]{1,0:T(8,128)(2,1)S(1)}, bf16[256,768]{1,0:T(8,128)(2,1)S(1)}, u32[]{:S(2)}, u32[]{:S(2)}) collective-permute-start(bf16[256,768]{1,0:T(8,128)(2,1)S(1)} %collective-permute-done.2), channel_id=1, source_target_pairs={{0,7},{1,0},{2,1},{3,2},{4,3},{5,4},{6,5},{7,6},{8,15},{9,8},{10,9... | collective-permute-start | bytes 1179656 | tf_op jit(solution)/shard_map/ppermute | solution.py:18
  109.7 26.1 %collective-permute-start.4 = (bf16[256,768]{1,0:T(8,128)(2,1)S(1)}, bf16[256,768]{1,0:T(8,128)(2,1)S(1)}, u32[]{:S(2)}, u32[]{:S(2)}) collective-permute-start(bf16[256,768]{1,0:T(8,128)(2,1)S(1)} %collective-permute-done.3), channel_id=1, source_target_pairs={{0,7},{1,0},{2,1},{3,2},{4,3},{5,4},{6,5},{7,6},{8,15},{9,8},{10,9... | collective-permute-start | bytes 1179656 | tf_op jit(solution)/shard_map/ppermute | solution.py:18
  113.4 308.2 %reduce-scatter.14.cloned.1.call-start = ((), (), s32[]{:S(2)}) async-start(), calls=%async_computation.14 | async-start | bytes 7077888 | tf_op jit(solution)/shard_map/reduce_scatter | solution.py:280
  135.7 10.2 %collective-permute-start.5 = (bf16[256,768]{1,0:T(8,128)(2,1)S(1)}, bf16[256,768]{1,0:T(8,128)(2,1)S(1)}, u32[]{:S(2)}, u32[]{:S(2)}) collective-permute-start(bf16[256,768]{1,0:T(8,128)(2,1)S(1)} %collective-permute-done.4), channel_id=1, source_target_pairs={{0,7},{1,0},{2,1},{3,2},{4,3},{5,4},{6,5},{7,6},{8,15},{9,8},{10,9... | collective-permute-start | bytes 1179656 | tf_op jit(solution)/shard_map/ppermute | solution.py:18
  145.9 12.4 %collective-permute-start.6 = (bf16[256,768]{1,0:T(8,128)(2,1)S(1)}, bf16[256,768]{1,0:T(8,128)(2,1)S(1)}, u32[]{:S(2)}, u32[]{:S(2)}) collective-permute-start(bf16[256,768]{1,0:T(8,128)(2,1)S(1)} %collective-permute-done.5), channel_id=1, source_target_pairs={{0,7},{1,0},{2,1},{3,2},{4,3},{5,4},{6,5},{7,6},{8,15},{9,8},{10,9... | collective-permute-start | bytes 1179656 | tf_op jit(solution)/shard_map/ppermute | solution.py:18
  353.0 103.0 %reduce-scatter.22.cloned.1.call-start = ((), (), s32[]{:S(2)}) async-start(), calls=%async_computation.18 | async-start | bytes 1327104
  357.0 132.8 %reduce-scatter.24.cloned.1.call-start = ((), (), s32[]{:S(2)}) async-start(), calls=%async_computation.19 | async-start | bytes 1327104
  424.7 98.7 %reduce-scatter.26.cloned.1.call-start = ((), (), s32[]{:S(2)}) async-start(), calls=%async_computation.20 | async-start | bytes 1327104
  426.8 130.1 %reduce-scatter.16.cloned.1.call-start = ((), (), s32[]{:S(2)}) async-start(), calls=%async_computation.15 | async-start | bytes 1327104 | tf_op jit(solution)/shard_map/reduce_scatter | solution.py:336
  428.4 183.9 %reduce-scatter.20.cloned.1.call-start = ((), (), s32[]{:S(2)}) async-start(), calls=%async_computation.17 | async-start | bytes 5308416 | tf_op jit(solution)/shard_map/reduce_scatter | solution.py:354
  433.8 234.0 %reduce-scatter.18.cloned.1.call-start = ((), (), s32[]{:S(2)}) async-start(), calls=%async_computation.16 | async-start | bytes 5308416 | tf_op jit(solution)/shard_map/reduce_scatter | solution.py:348
  440.1 230.6 %copy-start.12 = (f32[256,768]{1,0:T(8,128)S(1)}, f32[256,768]{1,0:T(8,128)}, u32[]{:S(2)}) copy-start(f32[256,768]{1,0:T(8,128)} %copy-done.11) | copy-start | bytes 2359300
  440.1 230.6 %copy-start.45 = (f32[256]{0:T(256)S(1)}, f32[256]{0:T(256)}, u32[]{:S(2)}) copy-start(f32[256]{0:T(256)} %copy-done.44) | copy-start | bytes 3076
  440.1 317.8 %all-reduce.23.cloned.1.call-start = ((), (), s32[]{:S(2)}) async-start(), calls=%async_computation.21 | async-start | bytes 3833856 | tf_op jit(solution)/shard_map/psum | solution.py:369
  (65 other events, 1704.1 us)
Sparse Core Ops, SparseCore 0:
  9.6 25.6 all-gather.8
  37.0 22.4 all-gather.12
  61.1 25.6 all-gather.14
  88.9 42.3 all-gather.10
  132.8 28.6 all-gather.16
  163.0 51.8 all-gather.18
  216.5 49.9 all-gather.20
  353.1 68.4 reduce-scatter.13
  424.5 31.4 reduce-scatter.21
  458.7 31.0 reduce-scatter.23
  492.1 31.2 reduce-scatter.25
  525.5 31.3 reduce-scatter.15
  559.2 53.0 reduce-scatter.19
  614.5 53.3 reduce-scatter.17
  672.1 66.5 all-reduce.22
